TPU v7x, 128 devices: a whole 4x4x4 slice. The times are simulated.
128 devices in a mesh: point: 32 (over z_hi, x, y), batch: 4 (over z_lo, core).
Axes of the slice: x: 4, y: 4, z: 4 (z_hi: 2, z_lo: 2; z = z_hi * 2 + z_lo), core: 2. Of those that a mesh axis runs over, the one named last changes fastest.
Arguments:
- activations: bfloat16 [128, 14, 14, 1024], P('batch'), may hold values from -8 to 8
- labels: int32 [128], P('batch'), may hold values from 0 to 999
- t_values: float32 [64], replicated, may hold values from 0 to 1
- point_index: int32 [32], replicated, may hold values from 0 to 63
- w_reduce: bfloat16 [3, 1024, 256], P(None, 'point'), may hold values from -1 to 1
- w_spatial: bfloat16 [3, 2304, 256], P(None, 'point'), may hold values from -0.125 to 0.125
- w_expand: bfloat16 [3, 256, 1024], P(None, 'point'), may hold values from -0.375 to 0.375
- w_classes: bfloat16 [3, 1000, 1024], P(None, None, 'point'), may hold values from -0.1875 to 0.1875
- norm_gain: float32 [3, 1536], replicated, may hold values from 0.5 to 1.5
- norm_bias: float32 [3, 1536], replicated, may hold values from -3 to 3
- class_bias: float32 [3, 1000], replicated, may hold values from -3 to 3
Outputs:
- mean_reduce: float32 [32, 256], P('point')
- var_reduce: float32 [32, 256], P('point')
- mean_spatial: float32 [32, 256], P('point')
- var_spatial: float32 [32, 256], P('point')
- mean_expand: float32 [32, 1024], P('point')
- var_expand: float32 [32, 1024], P('point')
- margin: float32 [32], replicated
All inputs are finite; a program needn't handle non-finite values.
Results may differ from a plain program's by a relative error of at most 0.003.
Values may be sent and summed in bfloat16 or wider, within the bound.
No kernel may reach another device: no remote copies, remote signals or barrier semaphores. Data moves between devices by JAX's collectives and lax.ppermute only.
A program may use at most 128 MiB of HBM per device.

v0:
```python
import jax
import jax.numpy as jnp
from jax import lax
from jax.sharding import Mesh
from jax.sharding import PartitionSpec as P

BATCH = ("batch_0", "batch_1")
EPSILON = 1e-05


def by_axis(x, axes):
    for axis in axes:
        x = lax.psum(x, axis)
    return x


def sent_to_all(x, axis):
    copies = jnp.broadcast_to(x, (lax.axis_size(axis), *x.shape))
    return lax.all_to_all(copies, axis, split_axis=0, concat_axis=0, tiled=True)


def over_copies(x, axis):
    everything = sent_to_all(x, axis)
    return jnp.sum(everything, axis=0)


def joined_along(blocks, dim):
    blocks = jnp.moveaxis(blocks, 0, dim)
    dims = blocks.shape
    return blocks.reshape(*dims[:dim], dims[dim] * dims[dim + 1], *dims[dim + 2 :])


def gather_directly(x, axis, dim):
    blocks = sent_to_all(x, axis)
    return joined_along(blocks, dim)


def curve_coefficients(t_values, point_index):
    table_size = t_values.shape[0]
    matches = point_index[:, None] == jnp.arange(table_size, dtype=jnp.int32)[None, :]
    picked = jnp.sum(jnp.where(matches, t_values[None, :], 0.0), axis=1)
    doubled = 2.0 * picked
    return jnp.stack(
        [
            jnp.maximum(1.0 - doubled, 0.0),
            1.0 - jnp.abs(1.0 - doubled),
            jnp.maximum(doubled - 1.0, 0.0),
        ],
        axis=1,
    )


def blend_all(coefficients, endpoints):
    target_shape = (coefficients.shape[0],) + (1,) * (endpoints.ndim - 1)
    start_part = coefficients[:, 0].reshape(target_shape) * endpoints[0].astype(jnp.float32)[None]
    bend_part = coefficients[:, 1].reshape(target_shape) * endpoints[1].astype(jnp.float32)[None]
    final_part = coefficients[:, 2].reshape(target_shape) * endpoints[2].astype(jnp.float32)[None]
    return start_part + bend_part + final_part


def point_weight(endpoints, coefficients, by_columns):
    all_points = blend_all(coefficients, endpoints).astype(jnp.bfloat16)
    if by_columns:
        received = lax.all_to_all(all_points, "point", split_axis=0, concat_axis=2, tiled=True)
    else:
        received = lax.all_to_all(all_points, "point", split_axis=0, concat_axis=1, tiled=True)
    return received[0]


def map_product(maps, kernel):
    return lax.dot_general(
        maps, kernel, (((3,), (0,)), ((), ())), preferred_element_type=jnp.float32
    )


def batch_norm(pre_norm, gain_part, bias_part, row_count):
    channel_total, channel_squares = (
        by_axis(jnp.sum(pre_norm, axis=(0, 1, 2)), BATCH),
        by_axis(jnp.sum(pre_norm * pre_norm, axis=(0, 1, 2)), BATCH),
    )
    channel_mean = channel_total / row_count
    channel_var = channel_squares / row_count - channel_mean * channel_mean
    scaled = (pre_norm - channel_mean) * lax.rsqrt(channel_var + EPSILON) * gain_part + bias_part
    return (channel_mean, channel_var, scaled)


def spatial_conv(source, kernel):
    side_len = source.shape[1]
    middle = source.shape[3]
    padded = jnp.pad(source, ((0, 0), (1, 1), (1, 1), (0, 0)))
    widened = jnp.concatenate(
        [
            padded[:, :, 0:side_len, :],
            padded[:, :, 1 : side_len + 1, :],
            padded[:, :, 2 : side_len + 2, :],
        ],
        axis=3,
    )
    summed = map_product(widened[:, 0:side_len], kernel[0 : 3 * middle])
    summed = summed + map_product(widened[:, 1 : side_len + 1], kernel[3 * middle : 6 * middle])
    summed = summed + map_product(widened[:, 2 : side_len + 2], kernel[6 * middle : 9 * middle])
    return summed


def shards(
    activations,
    labels,
    t_values,
    point_index,
    w_reduce,
    w_spatial,
    w_expand,
    w_classes,
    norm_gain,
    norm_bias,
    class_bias,
):
    coefficients = curve_coefficients(t_values, point_index)
    own_row = lax.dynamic_slice_in_dim(coefficients, lax.axis_index("point"), 1, 0)
    reduce_w = point_weight(w_reduce, coefficients, False)
    spatial_w = point_weight(w_spatial, coefficients, False)
    expand_w = point_weight(w_expand, coefficients, False)
    class_w = point_weight(w_classes, coefficients, True)
    gain_now = blend_all(own_row, norm_gain)[0]
    bias_now = blend_all(own_row, norm_bias)[0]
    shift_now = blend_all(own_row, class_bias)[0]
    images, side_len, _, channels = activations.shape
    middle = w_reduce.shape[2]
    row_count = float(images * side_len * side_len * lax.axis_size(BATCH))
    reduced = map_product(activations, reduce_w)
    mean_one, var_one, normed_one = batch_norm(
        reduced, gain_now[:middle], bias_now[:middle], row_count
    )
    first = jax.nn.relu(normed_one).astype(jnp.bfloat16)
    spatial = spatial_conv(first, spatial_w)
    mean_two, var_two, normed_two = batch_norm(
        spatial, gain_now[middle : 2 * middle], bias_now[middle : 2 * middle], row_count
    )
    second = jax.nn.relu(normed_two).astype(jnp.bfloat16)
    expanded = map_product(second, expand_w)
    mean_three, var_three, normed_three = batch_norm(
        expanded, gain_now[2 * middle :], bias_now[2 * middle :], row_count
    )
    block_out = jax.nn.relu(normed_three + activations.astype(jnp.float32))
    pooled = jnp.mean(block_out, axis=(1, 2)).astype(jnp.bfloat16)
    logits = (
        lax.dot_general(
            pooled, class_w, (((1,), (1,)), ((), ())), preferred_element_type=jnp.float32
        )
        + shift_now
    )
    classes = logits.shape[1]
    onehot = labels[:, None] == jnp.arange(classes, dtype=jnp.int32)[None, :]
    correct = jnp.sum(jnp.where(onehot, logits, 0.0), axis=1)
    rivals = jnp.max(jnp.where(onehot, -1e30, logits), axis=1)
    partial_value = jnp.sum(correct - rivals) / (images * lax.axis_size(BATCH))
    group_sum = over_copies(partial_value.reshape(1), BATCH)
    margin_all = gather_directly(group_sum, "point", 0)
    return (
        mean_one[None],
        var_one[None],
        mean_two[None],
        var_two[None],
        mean_three[None],
        var_three[None],
        margin_all,
    )


def solution(mesh):
    torus = Mesh(mesh.devices.reshape(mesh.shape["point"], 2, 2), ("point", "batch_0", "batch_1"))
    return jax.shard_map(
        shards,
        mesh=torus,
        in_specs=(
            P(BATCH, None, None, None),
            P(BATCH),
            P(),
            P(),
            P(None, "point", None),
            P(None, "point", None),
            P(None, "point", None),
            P(None, None, "point"),
            P(),
            P(),
            P(),
        ),
        out_specs=(
            P("point", None),
            P("point", None),
            P("point", None),
            P("point", None),
            P("point", None),
            P("point", None),
            P(),
        ),
        check_vma=False,
    )
```

profile of v0, /device:TPU:0, one launch (start us, length us, event | category | flops | bytes accessed | tf_op | source)
XLA Modules:
  0.0 189.2 jit_solution(16724359364042612514)
XLA Ops:
  0.6 0.8 bitcast_convert_fusion.11
  1.4 0.8 select_reduce_fusion.2
  2.3 1.1 add_convert_fusion.3
  3.3 10.7 %all-to-all-start = ((bf16[32,32,256]{2,1,0:T(8,128)(2,1)}), bf16[32,32,256]{2,1,0:T(8,128)(2,1)S(1)}, u32[]{:S(2)}, u32[]{:S(2)}) async-start(bf16[32,32,256]{2,1,0:T(8,128)(2,1)} %add_convert_fusion.3), calls=%async_computation | async-start | bytes 1048576 | tf_op jit(solution)/shard_map/all_to_all | solution.py:66
  14.1 0.1 constant_dynamic-slice_fusion
  14.2 0.5 fusion.17
  14.7 2.8 %multiply_add_fusion = (f32[1,1536]{1,0:T(1,128)S(1)}, f32[1,1536]{1,0:T(1,128)S(1)}) fusion(f32[3,1536]{1,0:T(4,128)} %param.20, f32[]{:T(128)} %bitcast.13, f32[]{:T(128)} %bitcast.12, f32[]{:T(128)} %bitcast.11, f32[3,1536]{1,0:T(4,128)} %param.19), kind=kLoop, calls=%fused_computation.48 | loop fusion | flops 15360 | bytes 49164 | tf_op jit(solution)/shard_map/add | solution.py:58
  17.6 0.8 bitcast_convert_fusion.5
  18.4 0.8 bitcast_convert_fusion.8
  19.1 2.8 %multiply_add_fusion.2 = f32[1,1000]{1,0:T(1,128)S(1)} fusion(f32[3,1000]{1,0:T(4,128)} %param.21, f32[]{:T(128)} %bitcast.13, f32[]{:T(128)} %bitcast.12, f32[]{:T(128)} %bitcast.11), kind=kLoop, calls=%fused_computation.50 | loop fusion | flops 5000 | bytes 16012 | tf_op jit(solution)/shard_map/add | solution.py:58
  21.9 0.9 bitcast_convert_fusion.2
  22.9 1.6 add_convert_fusion.1
  24.5 1.1 add_convert_fusion.2
  25.6 2.4 %add_convert_fusion = bf16[32,1000,32]{1,2,0:T(8,128)(2,1)} fusion(f32[1000,32]{0,1:T(8,128)S(1)} %get-tuple-element.37, f32[32]{0:T(128)S(1)} %get-tuple-element.60, f32[1000,32]{0,1:T(8,128)S(1)} %get-tuple-element.38, f32[32]{0:T(128)S(1)} %get-tuple-element.61, f32[1000,32]{0,1:T(8,128)S(1)} %get-tuple-element.36, f32[32]{0:T(128)S(1)} %get-tuple-element.62), kind=kLoop, calls=%fused_computation.8 | loop fusion | flops 6144000 | bytes 2432384 | tf_op jit(solution)/shard_map/convert_element_type | solution.py:62
  27.9 0.0 all-to-all-done
  27.9 9.8 %all-to-all-start.1 = ((bf16[32,72,256]{2,1,0:T(8,128)(2,1)}), bf16[32,72,256]{2,1,0:T(8,128)(2,1)S(1)}, u32[]{:S(2)}, u32[]{:S(2)}) async-start(bf16[32,72,256]{2,1,0:T(8,128)(2,1)} %add_convert_fusion.1), calls=%async_computation.1 | async-start | bytes 2359296 | tf_op jit(solution)/shard_map/all_to_all | solution.py:66
  37.8 10.8 %multiply_reduce_fusion.2 = (f32[256]{0:T(256)S(1)}, f32[256]{0:T(256)S(1)}, f32[256,32,14,14]{0,1,3,2:T(8,128)}) fusion(bf16[1024,256,1,1]{1,0,3,2:T(8,128)(2,1)S(1)} %bitcast.103, bf16[32,14,14,1024]{3,0,2,1:T(8,128)(2,1)} %param.11), kind=kOutput, calls=%fused_computation.7 | convolution fusion | flops 3293150720 | bytes 19793920 | tf_op jit(solution)/shard_map/dot_general | solution.py:71
  48.6 5.1 %all-reduce.6 = (f32[256]{0:T(256)S(1)}, f32[256]{0:T(256)S(1)}) all-reduce(f32[256]{0:T(256)S(1)} %get-tuple-element.12, f32[256]{0:T(256)S(1)} %get-tuple-element.11), channel_id=1, replica_groups=mesh['point'=32,'batch_0'=2,'batch_1'=2] {'batch_0'}, use_global_device_ids=true, to_apply=%region_2.3 | all-reduce | flops 512 | bytes 4096 | tf_op jit(solution)/shard_map/psum | solution.py:13
  53.8 2.4 %all-reduce.3 = (f32[256]{0:T(256)S(1)}, f32[256]{0:T(256)S(1)}) all-reduce(f32[256]{0:T(256)S(1)} %get-tuple-element.25, f32[256]{0:T(256)S(1)} %get-tuple-element.26), channel_id=1, replica_groups=mesh['point'=32,'batch_0'=2,'batch_1'=2] {'batch_1'}, use_global_device_ids=true, to_apply=%region_3.4 | all-reduce | flops 512 | bytes 4096 | tf_op jit(solution)/shard_map/psum | solution.py:13
  56.2 0.6 add_rsqrt_fusion.2
  56.8 4.1 %fusion.1 = bf16[32,14,14,256]{3,0,2,1:T(8,128)(2,1)S(1)} fusion(f32[256,32,14,14]{0,1,3,2:T(8,128)} %get-tuple-element.63, f32[256]{0:T(256)S(1)} %bitcast.110, f32[256]{0:T(256)S(1)} %bitcast.111, f32[256]{0:T(256)S(1)} %get-tuple-element.31, f32[256]{0:T(256)S(1)} %get-tuple-element.57), kind=kLoop, calls=%fused_computation.13 | loop fusion | flops 9633792 | bytes 9637888 | tf_op jit(solution)/shard_map/convert_element_type | solution.py:134
  60.8 4.9 %pad_slice_fusion.2 = (bf16[32,16,14,256]{3,0,2,1:T(8,128)(2,1)}, bf16[32,16,14,256]{3,0,2,1:T(8,128)(2,1)}, bf16[32,16,14,256]{3,0,2,1:T(8,128)(2,1)}) fusion(bf16[32,14,14,256]{3,0,2,1:T(8,128)(2,1)S(1)} %fusion.1), kind=kLoop, calls=%fused_computation.11 | loop fusion | bytes 14221312 | tf_op jit(solution)/shard_map/slice | solution.py:93
  65.8 0.0 all-to-all-done.1
  65.8 9.8 %all-to-all-start.2 = ((bf16[32,8,1024]{2,1,0:T(8,128)(2,1)}), bf16[32,8,1024]{2,1,0:T(8,128)(2,1)S(1)}, u32[]{:S(2)}, u32[]{:S(2)}) async-start(bf16[32,8,1024]{2,1,0:T(8,128)(2,1)} %add_convert_fusion.2), calls=%async_computation.2 | async-start | bytes 1048576 | tf_op jit(solution)/shard_map/all_to_all | solution.py:66
  75.6 7.3 %fusion.9 = f32[32,14,14,256]{3,0,2,1:T(8,128)} fusion(bf16[2304,256]{1,0:T(8,128)(2,1)S(1)} %bitcast.100, bf16[32,16,14,256]{3,0,2,1:T(8,128)(2,1)} %get-tuple-element.35, bf16[32,16,14,256]{3,0,2,1:T(8,128)(2,1)} %get-tuple-element.34, bf16[32,16,14,256]{3,0,2,1:T(8,128)(2,1)} %get-tuple-element.33), kind=kOutput, calls=%fused_computation.28 | convolution fusion | flops 2499280896 | bytes 17825792 | tf_op jit(solution)/shard_map/dot_general | solution.py:71
  82.9 1.1 copy-done.1
  83.9 1.0 copy-done.2
  85.0 5.4 %fusion.8 = f32[32,14,14,256]{3,0,2,1:T(8,128)} fusion(bf16[2304,256]{1,0:T(8,128)(2,1)S(1)} %bitcast.101, bf16[32,16,14,256]{3,0,2,1:T(8,128)(2,1)S(1)} %copy-done.2, bf16[32,16,14,256]{3,0,2,1:T(8,128)(2,1)S(1)} %copy-done.1, bf16[32,16,14,256]{3,0,2,1:T(8,128)(2,1)S(1)} %copy-done), kind=kOutput, calls=%fused_computation.26 | convolution fusion | flops 2499280896 | bytes 17825792 | tf_op jit(solution)/shard_map/dot_general | solution.py:71
  90.4 8.9 %multiply_reduce_fusion.1 = (f32[256]{0:T(256)S(1)}, f32[256]{0:T(256)S(1)}, f32[32,14,14,256]{3,0,2,1:T(8,128)}) fusion(bf16[2304,256]{1,0:T(8,128)(2,1)S(1)} %bitcast.102, bf16[32,16,14,256]{3,0,2,1:T(8,128)(2,1)S(1)} %copy-done.2, bf16[32,16,14,256]{3,0,2,1:T(8,128)(2,1)S(1)} %copy-done.1, bf16[32,16,14,256]{3,0,2,1:T(8,128)(2,1)S(1)} %copy-done, ...), kind=kOutput, calls=%fused_computation.5 | convolution fusion | flops 2507308544 | bytes 30672896 | tf_op jit(solution)/shard_map/dot_general | solution.py:71
  99.3 4.9 %all-reduce.5 = (f32[256]{0:T(256)S(1)}, f32[256]{0:T(256)S(1)}) all-reduce(f32[256]{0:T(256)S(1)} %get-tuple-element.10, f32[256]{0:T(256)S(1)} %get-tuple-element.9), channel_id=1, replica_groups=mesh['point'=32,'batch_0'=2,'batch_1'=2] {'batch_0'}, use_global_device_ids=true, to_apply=%region_8.9 | all-reduce | flops 512 | bytes 4096 | tf_op jit(solution)/shard_map/psum | solution.py:13
  104.2 2.4 %all-reduce.2 = (f32[256]{0:T(256)S(1)}, f32[256]{0:T(256)S(1)}) all-reduce(f32[256]{0:T(256)S(1)} %get-tuple-element.23, f32[256]{0:T(256)S(1)} %get-tuple-element.24), channel_id=1, replica_groups=mesh['point'=32,'batch_0'=2,'batch_1'=2] {'batch_1'}, use_global_device_ids=true, to_apply=%region_9.10 | all-reduce | flops 512 | bytes 4096 | tf_op jit(solution)/shard_map/psum | solution.py:13
  106.7 0.6 add_rsqrt_fusion.1
  107.3 0.0 all-to-all-done.2
  107.3 9.6 %all-to-all-start.3 = ((bf16[32,1000,32]{1,2,0:T(8,128)(2,1)}), bf16[32,1000,32]{1,2,0:T(8,128)(2,1)S(1)}, u32[]{:S(2)}, u32[]{:S(2)}) async-start(bf16[32,1000,32]{1,2,0:T(8,128)(2,1)} %add_convert_fusion), calls=%async_computation.3 | async-start | bytes 4194304 | tf_op jit(solution)/shard_map/all_to_all | solution.py:64
  116.9 14.0 %multiply_reduce_fusion = (f32[1024]{0:T(1024)S(1)}, f32[1024]{0:T(1024)S(1)}, f32[32,14,14,1024]{3,0,2,1:T(8,128)}) fusion(bf16[32,8,1024]{2,1,0:T(8,128)(2,1)S(1)} %all-to-all-done.2, f32[32,14,14,256]{3,0,2,1:T(8,128)} %get-tuple-element.64, f32[256]{0:T(256)S(1)} %bitcast.116, f32[256]{0:T(256)S(1)} %bitcast.117, f32[256]{0:T(256)S(1)} %get-tuple-element.29, ...), kind=kOutput, calls=%fused_computation.1 | convolution fusion | flops 3317233664 | bytes 32649216 | tf_op jit(solution)/shard_map/dot_general | solution.py:71
  130.9 5.0 %all-reduce.4 = (f32[1024]{0:T(1024)S(1)}, f32[1024]{0:T(1024)S(1)}) all-reduce(f32[1024]{0:T(1024)S(1)} %get-tuple-element.8, f32[1024]{0:T(1024)S(1)} %get-tuple-element.7), channel_id=1, replica_groups=mesh['point'=32,'batch_0'=2,'batch_1'=2] {'batch_0'}, use_global_device_ids=true, to_apply=%region_14.15 | all-reduce | flops 2048 | bytes 16384 | tf_op jit(solution)/shard_map/psum | solution.py:13
  135.9 2.5 %all-reduce.1 = (f32[1024]{0:T(1024)S(1)}, f32[1024]{0:T(1024)S(1)}) all-reduce(f32[1024]{0:T(1024)S(1)} %get-tuple-element.21, f32[1024]{0:T(1024)S(1)} %get-tuple-element.22), channel_id=1, replica_groups=mesh['point'=32,'batch_0'=2,'batch_1'=2] {'batch_1'}, use_global_device_ids=true, to_apply=%region_15.16 | all-reduce | flops 2048 | bytes 16384 | tf_op jit(solution)/shard_map/psum | solution.py:13
  138.4 0.6 add_rsqrt_fusion
  139.0 14.7 %maximum_reduce_fusion = f32[32,1024]{1,0:T(8,128)S(1)} fusion(bf16[32,14,14,1024]{3,0,2,1:T(8,128)(2,1)} %param.11, f32[32,14,14,1024]{3,0,2,1:T(8,128)} %get-tuple-element.65, f32[1024]{0:T(1024)S(1)} %bitcast.106, f32[1024]{0:T(1024)S(1)} %bitcast.107, f32[1024]{0:T(1024)S(1)} %get-tuple-element.27, f32[1024]{0:T(1024)S(1)} %get-tuple-element.52), kind=kLoop, calls=%fused_computation | loop fusion | flops 51347456 | bytes 38682624 | tf_op jit(solution)/shard_map/reduce_sum | solution.py:145
  153.7 0.0 copy-done.3
  153.7 0.0 all-to-all-done.3
  153.8 0.6 select_reduce_fusion
  154.4 0.6 subtract_reduce_fusion
  155.6 6.3 %all_to_all.54 = f32[4,1,1]{2,1,0:T(1,128)S(1)} all-to-all(f32[4,1,1]{2,1,0:T(1,128)S(1)} %broadcast_in_dim.46), channel_id=1, replica_groups=mesh['point'=32,'batch_0'=2,'batch_1'=2] {'batch_0','batch_1'}, dimensions={0} | all-to-all | bytes 32 | tf_op jit(solution)/shard_map/all_to_all | solution.py:19
  161.9 0.6 reduce_sum.109
  162.5 0.7 broadcast_in_dim.47
  163.2 25.2 %all_to_all.55 = f32[32,1,1]{2,1,0:T(1,128)S(1)} all-to-all(f32[32,1,1]{2,1,0:T(1,128)S(1)} %broadcast_in_dim.47), channel_id=1, replica_groups=mesh['point'=32,'batch_0'=2,'batch_1'=2] {'point'}, dimensions={0} | all-to-all | bytes 256 | tf_op jit(solution)/shard_map/all_to_all | solution.py:19
  188.4 0.8 reduce.4
  (18 shorter events, 0.1 us)
Async XLA Ops:
  3.3 24.6 %all-to-all-start = ((bf16[32,32,256]{2,1,0:T(8,128)(2,1)}), bf16[32,32,256]{2,1,0:T(8,128)(2,1)S(1)}, u32[]{:S(2)}, u32[]{:S(2)}) async-start(bf16[32,32,256]{2,1,0:T(8,128)(2,1)} %add_convert_fusion.3), calls=%async_computation | async-start | bytes 1048576 | tf_op jit(solution)/shard_map/all_to_all | solution.py:66
  27.9 37.8 %all-to-all-start.1 = ((bf16[32,72,256]{2,1,0:T(8,128)(2,1)}), bf16[32,72,256]{2,1,0:T(8,128)(2,1)S(1)}, u32[]{:S(2)}, u32[]{:S(2)}) async-start(bf16[32,72,256]{2,1,0:T(8,128)(2,1)} %add_convert_fusion.1), calls=%async_computation.1 | async-start | bytes 2359296 | tf_op jit(solution)/shard_map/all_to_all | solution.py:66
  56.8 9.0 %copy-start.4 = (f32[256]{0:T(256)}, f32[256]{0:T(256)S(1)}, u32[]{:S(2)}) copy-start(f32[256]{0:T(256)S(1)} %get-tuple-element.57) | copy-start | bytes 3076
  65.8 41.5 %all-to-all-start.2 = ((bf16[32,8,1024]{2,1,0:T(8,128)(2,1)}), bf16[32,8,1024]{2,1,0:T(8,128)(2,1)S(1)}, u32[]{:S(2)}, u32[]{:S(2)}) async-start(bf16[32,8,1024]{2,1,0:T(8,128)(2,1)} %add_convert_fusion.2), calls=%async_computation.2 | async-start | bytes 1048576 | tf_op jit(solution)/shard_map/all_to_all | solution.py:66
  75.6 7.3 %copy-start = (bf16[32,16,14,256]{3,0,2,1:T(8,128)(2,1)S(1)}, bf16[32,16,14,256]{3,0,2,1:T(8,128)(2,1)}, u32[]{:S(2)}) copy-start(bf16[32,16,14,256]{3,0,2,1:T(8,128)(2,1)} %get-tuple-element.33) | copy-start | bytes 11010052
  75.6 8.4 %copy-start.1 = (bf16[32,16,14,256]{3,0,2,1:T(8,128)(2,1)S(1)}, bf16[32,16,14,256]{3,0,2,1:T(8,128)(2,1)}, u32[]{:S(2)}) copy-start(bf16[32,16,14,256]{3,0,2,1:T(8,128)(2,1)} %get-tuple-element.34) | copy-start | bytes 11010052
  75.6 9.4 %copy-start.2 = (bf16[32,16,14,256]{3,0,2,1:T(8,128)(2,1)S(1)}, bf16[32,16,14,256]{3,0,2,1:T(8,128)(2,1)}, u32[]{:S(2)}) copy-start(bf16[32,16,14,256]{3,0,2,1:T(8,128)(2,1)} %get-tuple-element.35) | copy-start | bytes 11010052
  107.2 23.7 %copy-start.5 = (f32[256]{0:T(256)}, f32[256]{0:T(256)S(1)}, u32[]{:S(2)}) copy-start(f32[256]{0:T(256)S(1)} %get-tuple-element.56) | copy-start | bytes 3076
  107.3 46.5 %all-to-all-start.3 = ((bf16[32,1000,32]{1,2,0:T(8,128)(2,1)}), bf16[32,1000,32]{1,2,0:T(8,128)(2,1)S(1)}, u32[]{:S(2)}, u32[]{:S(2)}) async-start(bf16[32,1000,32]{1,2,0:T(8,128)(2,1)} %add_convert_fusion), calls=%async_computation.3 | async-start | bytes 4194304 | tf_op jit(solution)/shard_map/all_to_all | solution.py:64
  139.0 14.8 %copy-start.3 = (f32[1024]{0:T(1024)}, f32[1024]{0:T(1024)S(1)}, u32[]{:S(2)}) copy-start(f32[1024]{0:T(1024)S(1)} %get-tuple-element.52) | copy-start | bytes 12292
  139.0 14.8 %copy-start.6 = (s32[32]{0:T(128)S(1)}, s32[32]{0:T(128)}, u32[]{:S(2)}) copy-start(s32[32]{0:T(128)} %param.12) | copy-start | bytes 388
where the time goes:
time: 190 us; the launch traced here: 189 us
  blocking collectives  53.9 us (28%)
  matrix products  47.1 us (25%)
  starting transfers between devices  40 us (21%)
  other arithmetic  38.5 us (20%)
  local copies, waits for them, and re-layouts  8.33 us (4%)
    dot_general x5, matrix products, map_product(): lax.dot_general(maps, kernel, (((3,), (0,)), ((), ())), preferred_element...  46.5 us
    all_to_all x2, blocking collectives, sent_to_all(): return lax.all_to_all(copies, axis, split_axis=0, concat_axis=0, tiled=True)  31.5 us
    all_to_all x3, starting transfers between devices, point_weight(): lax.all_to_all(all_points, 'point', split_axis=0, concat_axis=1, tiled=True)  30.3 us
    psum x6, blocking collectives, by_axis(): x = lax.psum(x, axis)  22.4 us
    reduce_sum x1, other arithmetic, shards(): pooled = jnp.mean(block_out, axis=(1, 2)).astype(jnp.bfloat16)  14.7 us
    all_to_all x1, starting transfers between devices, point_weight(): lax.all_to_all(all_points, 'point', split_axis=0, concat_axis=2, tiled=True)  9.65 us
    convert_element_type x4, other arithmetic, point_weight(): all_points = blend_all(coefficients, endpoints).astype(jnp.bfloat16)  6.13 us
    add x2, other arithmetic, blend_all(): return start_part + bend_part + final_part  5.61 us
  transfers between devices with their start and end apart: 4, of which 0 were waited for; matrix products, arithmetic and copies ran while one was open for 45% of the time, Pallas kernels for 0%

commit v1 on v0

--- a/solution.py
+++ b/solution.py
@@ -10,7 +10,7 @@
 
 def by_axis(x, axes):
     for axis in axes:
-        x = lax.psum(x, axis)
+        x = jnp.sum(lax.all_gather(x, axis), axis=0)
     return x
 
 

time: 190 us -> 206 us (1.084)
  starting transfers between devices: 40 us -> 56.3 us
  blocking collectives: 53.9 us -> 42.9 us
  waiting for transfers between devices: 0.01 us -> 9.09 us
    all_gather x0 -> x12, blocking collectives: none -> 36.8 us  [by_axis(): x = jnp.sum(lax.all_gather(x, axis), axis=0)]
    all_to_all x2 -> x1, blocking collectives: 31.5 us -> 6.12 us  [sent_to_all(): return lax.all_to_all(copies, axis, split_axis=0, concat_axis=0, tiled=True)]
    psum x6 -> x0, blocking collectives: 22.4 us -> none  [by_axis(): x = lax.psum(x, axis)]
    all_to_all x0 -> x1, starting transfers between devices: none -> 16.1 us  [sent_to_all(): return lax.all_to_all(copies, axis, split_axis=0, concat_axis=0, tiled=True)]
    all_to_all x0 -> x1, waiting for transfers between devices: none -> 9.07 us  [sent_to_all(): return lax.all_to_all(copies, axis, split_axis=0, concat_axis=0, tiled=True)]
  transfers between devices with their start and end apart: 4 -> 5, of which waited for: 0 -> 1; matrix products, arithmetic and copies ran while one was open for 45% -> 42% of each run, Pallas kernels for 0% -> 0%
where the time goes in v1:
time: 206 us; the launch traced here: 205 us
  starting transfers between devices  56.3 us (27%)
  matrix products  47 us (23%)
  blocking collectives  42.9 us (21%)
  other arithmetic  38.7 us (19%)
  waiting for transfers between devices  9.09 us (4%)
  local copies, waits for them, and re-layouts  8.97 us (4%)
    dot_general x5, matrix products, map_product(): lax.dot_general(maps, kernel, (((3,), (0,)), ((), ())), preferred_element...  46.5 us
    all_gather x12, blocking collectives, by_axis(): x = jnp.sum(lax.all_gather(x, axis), axis=0)  36.8 us
    all_to_all x3, starting transfers between devices, point_weight(): lax.all_to_all(all_points, 'point', split_axis=0, concat_axis=1, tiled=True)  30.6 us
    all_to_all x1, starting transfers between devices, sent_to_all(): return lax.all_to_all(copies, axis, split_axis=0, concat_axis=0, tiled=True)  16.1 us
    reduce_sum x1, other arithmetic, shards(): pooled = jnp.mean(block_out, axis=(1, 2)).astype(jnp.bfloat16)  14.7 us
    all_to_all x1, starting transfers between devices, point_weight(): lax.all_to_all(all_points, 'point', split_axis=0, concat_axis=2, tiled=True)  9.67 us
    all_to_all x1, waiting for transfers between devices, sent_to_all(): return lax.all_to_all(copies, axis, split_axis=0, concat_axis=0, tiled=True)  9.07 us
    convert_element_type x4, other arithmetic, point_weight(): all_points = blend_all(coefficients, endpoints).astype(jnp.bfloat16)  6.13 us
  transfers between devices with their start and end apart: 5, of which 1 were waited for; matrix products, arithmetic and copies ran while one was open for 42% of the time, Pallas kernels for 0%

profile of v1, /device:TPU:0, one launch (start us, length us, event | category | flops | bytes accessed | tf_op | source)
XLA Modules:
  0.0 204.5 jit_solution(147930060812155955)
XLA Ops:
  0.6 0.8 bitcast_convert_fusion.11
  1.4 0.8 select_reduce_fusion.2
  2.3 1.1 add_convert_fusion.3
  3.3 10.7 %all-to-all-start = ((bf16[32,32,256]{2,1,0:T(8,128)(2,1)}), bf16[32,32,256]{2,1,0:T(8,128)(2,1)S(1)}, u32[]{:S(2)}, u32[]{:S(2)}) async-start(bf16[32,32,256]{2,1,0:T(8,128)(2,1)} %add_convert_fusion.3), calls=%async_computation | async-start | bytes 1048576 | tf_op jit(solution)/shard_map/all_to_all | solution.py:66
  14.7 2.8 %multiply_add_fusion = (f32[1,1536]{1,0:T(1,128)S(1)}, f32[1,1536]{1,0:T(1,128)S(1)}) fusion(f32[3,1536]{1,0:T(4,128)} %param.20, f32[]{:T(128)} %bitcast.17, f32[]{:T(128)} %bitcast.16, f32[]{:T(128)} %bitcast.15, f32[3,1536]{1,0:T(4,128)} %param.19), kind=kLoop, calls=%fused_computation.48 | loop fusion | flops 15360 | bytes 49164 | tf_op jit(solution)/shard_map/add | solution.py:58
  17.6 0.8 bitcast_convert_fusion.5
  18.4 0.8 bitcast_convert_fusion.8
  19.1 2.8 %multiply_add_fusion.2 = f32[1,1000]{1,0:T(1,128)S(1)} fusion(f32[3,1000]{1,0:T(4,128)} %param.21, f32[]{:T(128)} %bitcast.17, f32[]{:T(128)} %bitcast.16, f32[]{:T(128)} %bitcast.15), kind=kLoop, calls=%fused_computation.50 | loop fusion | flops 5000 | bytes 16012 | tf_op jit(solution)/shard_map/add | solution.py:58
  21.9 0.9 bitcast_convert_fusion.2
  22.9 1.6 add_convert_fusion.1
  24.5 1.1 add_convert_fusion.2
  25.6 2.4 %add_convert_fusion = bf16[32,1000,32]{1,2,0:T(8,128)(2,1)} fusion(f32[1000,32]{0,1:T(8,128)S(1)} %get-tuple-element.19, f32[32]{0:T(128)S(1)} %get-tuple-element.48, f32[1000,32]{0,1:T(8,128)S(1)} %get-tuple-element.20, f32[32]{0:T(128)S(1)} %get-tuple-element.49, f32[1000,32]{0,1:T(8,128)S(1)} %get-tuple-element.18, f32[32]{0:T(128)S(1)} %get-tuple-element.50), kind=kLoop, calls=%fused_computation.8 | loop fusion | flops 6144000 | bytes 2432384 | tf_op jit(solution)/shard_map/convert_element_type | solution.py:62
  27.9 9.8 %all-to-all-start.1 = ((bf16[32,72,256]{2,1,0:T(8,128)(2,1)}), bf16[32,72,256]{2,1,0:T(8,128)(2,1)S(1)}, u32[]{:S(2)}, u32[]{:S(2)}) async-start(bf16[32,72,256]{2,1,0:T(8,128)(2,1)} %add_convert_fusion.1), calls=%async_computation.1 | async-start | bytes 2359296 | tf_op jit(solution)/shard_map/all_to_all | solution.py:66
  37.8 10.8 %multiply_reduce_fusion.2 = (f32[256]{0:T(256)S(1)}, f32[256]{0:T(256)S(1)}, f32[256,32,14,14]{0,1,3,2:T(8,128)}) fusion(bf16[1024,256,1,1]{1,0,3,2:T(8,128)(2,1)S(1)} %bitcast.111, bf16[32,14,14,1024]{3,0,2,1:T(8,128)(2,1)} %param.11), kind=kOutput, calls=%fused_computation.7 | convolution fusion | flops 3293150720 | bytes 19793920 | tf_op jit(solution)/shard_map/dot_general | solution.py:71
  48.6 4.2 %all-gather.12 = f32[2,1,256]{2,1,0:T(1,128)S(1)} all-gather(f32[1,1,256]{2,1,0:T(1,128)S(1)} %bitcast.134), channel_id=2, replica_groups=mesh['point'=32,'batch_0'=2,'batch_1'=2] {'batch_0'}, dimensions={0}, use_global_device_ids=true | all-gather | bytes 3072 | tf_op jit(solution)/shard_map/all_gather | solution.py:13
  52.9 1.8 all-gather.13
  54.7 4.2 %all-gather.14 = f32[2,1,256]{2,1,0:T(1,128)S(1)} all-gather(f32[1,1,256]{2,1,0:T(1,128)S(1)} %bitcast.132), channel_id=4, replica_groups=mesh['point'=32,'batch_0'=2,'batch_1'=2] {'batch_0'}, dimensions={0}, use_global_device_ids=true | all-gather | bytes 3072 | tf_op jit(solution)/shard_map/all_gather | solution.py:13
  59.0 1.8 all-gather.15
  60.8 0.6 multiply_subtract_fusion.2
  61.4 4.1 %fusion.1 = bf16[32,14,14,256]{3,0,2,1:T(8,128)(2,1)S(1)} fusion(f32[256,32,14,14]{0,1,3,2:T(8,128)} %get-tuple-element.51, f32[256]{0:T(256)S(1)} %bitcast.121, f32[256]{0:T(256)S(1)} %bitcast.122, f32[256]{0:T(256)S(1)} %get-tuple-element.43, f32[256]{0:T(256)S(1)} %get-tuple-element.45), kind=kLoop, calls=%fused_computation.13 | loop fusion | flops 9633792 | bytes 9637888 | tf_op jit(solution)/shard_map/convert_element_type | solution.py:134
  65.4 4.9 %pad_slice_fusion.2 = (bf16[32,16,14,256]{3,0,2,1:T(8,128)(2,1)}, bf16[32,16,14,256]{3,0,2,1:T(8,128)(2,1)}, bf16[32,16,14,256]{3,0,2,1:T(8,128)(2,1)}) fusion(bf16[32,14,14,256]{3,0,2,1:T(8,128)(2,1)S(1)} %fusion.1), kind=kLoop, calls=%fused_computation.11 | loop fusion | bytes 14221312 | tf_op jit(solution)/shard_map/slice | solution.py:93
  70.4 10.0 %all-to-all-start.2 = ((bf16[32,8,1024]{2,1,0:T(8,128)(2,1)}), bf16[32,8,1024]{2,1,0:T(8,128)(2,1)S(1)}, u32[]{:S(2)}, u32[]{:S(2)}) async-start(bf16[32,8,1024]{2,1,0:T(8,128)(2,1)} %add_convert_fusion.2), calls=%async_computation.2 | async-start | bytes 1048576 | tf_op jit(solution)/shard_map/all_to_all | solution.py:66
  80.4 7.3 %fusion.9 = f32[32,14,14,256]{3,0,2,1:T(8,128)} fusion(bf16[2304,256]{1,0:T(8,128)(2,1)S(1)} %bitcast.108, bf16[32,16,14,256]{3,0,2,1:T(8,128)(2,1)} %get-tuple-element.17, bf16[32,16,14,256]{3,0,2,1:T(8,128)(2,1)} %get-tuple-element.16, bf16[32,16,14,256]{3,0,2,1:T(8,128)(2,1)} %get-tuple-element.15), kind=kOutput, calls=%fused_computation.28 | convolution fusion | flops 2499280896 | bytes 17825792 | tf_op jit(solution)/shard_map/dot_general | solution.py:71
  87.7 1.1 copy-done.1
  88.8 1.0 copy-done.2
  89.8 5.4 %fusion.8 = f32[32,14,14,256]{3,0,2,1:T(8,128)} fusion(bf16[2304,256]{1,0:T(8,128)(2,1)S(1)} %bitcast.109, bf16[32,16,14,256]{3,0,2,1:T(8,128)(2,1)S(1)} %copy-done.2, bf16[32,16,14,256]{3,0,2,1:T(8,128)(2,1)S(1)} %copy-done.1, bf16[32,16,14,256]{3,0,2,1:T(8,128)(2,1)S(1)} %copy-done), kind=kOutput, calls=%fused_computation.26 | convolution fusion | flops 2499280896 | bytes 17825792 | tf_op jit(solution)/shard_map/dot_general | solution.py:71
  95.2 8.9 %multiply_reduce_fusion.1 = (f32[256]{0:T(256)S(1)}, f32[256]{0:T(256)S(1)}, f32[32,14,14,256]{3,0,2,1:T(8,128)}) fusion(bf16[2304,256]{1,0:T(8,128)(2,1)S(1)} %bitcast.110, bf16[32,16,14,256]{3,0,2,1:T(8,128)(2,1)S(1)} %copy-done.2, bf16[32,16,14,256]{3,0,2,1:T(8,128)(2,1)S(1)} %copy-done.1, bf16[32,16,14,256]{3,0,2,1:T(8,128)(2,1)S(1)} %copy-done, ...), kind=kOutput, calls=%fused_computation.5 | convolution fusion | flops 2507308544 | bytes 30672896 | tf_op jit(solution)/shard_map/dot_general | solution.py:71
  104.1 4.2 %all-gather.16 = f32[2,1,256]{2,1,0:T(1,128)S(1)} all-gather(f32[1,1,256]{2,1,0:T(1,128)S(1)} %bitcast.133), channel_id=6, replica_groups=mesh['point'=32,'batch_0'=2,'batch_1'=2] {'batch_0'}, dimensions={0}, use_global_device_ids=true | all-gather | bytes 3072 | tf_op jit(solution)/shard_map/all_gather | solution.py:13
  108.4 1.8 all-gather.17
  110.2 4.2 %all-gather.18 = f32[2,1,256]{2,1,0:T(1,128)S(1)} all-gather(f32[1,1,256]{2,1,0:T(1,128)S(1)} %bitcast.131), channel_id=8, replica_groups=mesh['point'=32,'batch_0'=2,'batch_1'=2] {'batch_0'}, dimensions={0}, use_global_device_ids=true | all-gather | bytes 3072 | tf_op jit(solution)/shard_map/all_gather | solution.py:13
  114.5 1.8 all-gather.19
  116.3 9.7 %all-to-all-start.3 = ((bf16[32,1000,32]{1,2,0:T(8,128)(2,1)}), bf16[32,1000,32]{1,2,0:T(8,128)(2,1)S(1)}, u32[]{:S(2)}, u32[]{:S(2)}) async-start(bf16[32,1000,32]{1,2,0:T(8,128)(2,1)} %add_convert_fusion), calls=%async_computation.3 | async-start | bytes 4194304 | tf_op jit(solution)/shard_map/all_to_all | solution.py:64
  126.0 14.0 %multiply_reduce_fusion = (f32[1024]{0:T(1024)S(1)}, f32[1024]{0:T(1024)S(1)}, f32[32,14,14,1024]{3,0,2,1:T(8,128)}) fusion(bf16[32,8,1024]{2,1,0:T(8,128)(2,1)S(1)} %all-to-all-done.2, f32[32,14,14,256]{3,0,2,1:T(8,128)} %get-tuple-element.52, f32[256]{0:T(256)S(1)} %bitcast.135, f32[256]{0:T(256)S(1)} %bitcast.136, f32[256]{0:T(256)S(1)} %get-tuple-element.40, ...), kind=kOutput, calls=%fused_computation.1 | convolution fusion | flops 3317233664 | bytes 32649216 | tf_op jit(solution)/shard_map/dot_general | solution.py:71
  140.0 4.4 %all-gather.8 = f32[2048]{0:T(1024)S(1)} all-gather(f32[1024]{0:T(1024)S(1)} %get-tuple-element.8), channel_id=10, replica_groups=mesh['point'=32,'batch_0'=2,'batch_1'=2] {'batch_0'}, dimensions={0}, use_global_device_ids=true | all-gather | bytes 12288 | tf_op jit(solution)/shard_map/all_gather | solution.py:13
  144.4 1.8 all-gather.9
  146.3 4.6 %all-gather.10 = f32[2048]{0:T(1024)S(1)} all-gather(f32[1024]{0:T(1024)S(1)} %get-tuple-element.7), channel_id=12, replica_groups=mesh['point'=32,'batch_0'=2,'batch_1'=2] {'batch_0'}, dimensions={0}, use_global_device_ids=true | all-gather | bytes 12288 | tf_op jit(solution)/shard_map/all_gather | solution.py:13
  150.9 1.8 all-gather.11
  152.8 0.6 multiply_subtract_fusion
  153.4 14.7 %maximum_reduce_fusion = f32[32,1024]{1,0:T(8,128)S(1)} fusion(bf16[32,14,14,1024]{3,0,2,1:T(8,128)(2,1)} %param.11, f32[32,14,14,1024]{3,0,2,1:T(8,128)} %get-tuple-element.53, f32[1024]{0:T(1024)S(1)} %bitcast.115, f32[1024]{0:T(1024)S(1)} %bitcast.116, f32[1024]{0:T(1024)S(1)} %get-tuple-element.34, f32[1024]{0:T(1024)S(1)} %get-tuple-element.36), kind=kLoop, calls=%fused_computation | loop fusion | flops 51347456 | bytes 38682624 | tf_op jit(solution)/shard_map/reduce_sum | solution.py:145
  168.1 0.6 select_reduce_fusion
  168.7 0.6 subtract_reduce_fusion
  170.0 6.1 %all_to_all.54 = f32[4,1,1]{2,1,0:T(1,128)S(1)} all-to-all(f32[4,1,1]{2,1,0:T(1,128)S(1)} %broadcast_in_dim.26), channel_id=1, replica_groups=mesh['point'=32,'batch_0'=2,'batch_1'=2] {'batch_0','batch_1'}, dimensions={0} | all-to-all | bytes 32 | tf_op jit(solution)/shard_map/all_to_all | solution.py:19
  176.1 0.6 reduce_sum.229
  176.7 1.2 broadcast_in_dim.27
  178.0 16.1 %all-to-all-start.5 = ((f32[32,1,1]{2,1,0:T(1,128)}), f32[32,1,1]{2,1,0:T(1,128)S(1)}, u32[]{:S(2)}, u32[]{:S(2)}) async-start(f32[32,1,1]{2,1,0:T(1,128)} %broadcast_in_dim.27), calls=%async_computation.5 | async-start | bytes 32768 | tf_op jit(solution)/shard_map/all_to_all | solution.py:19
  194.1 0.6 multiply_subtract_fusion.1
  194.6 9.1 %all-to-all-done.5 = f32[32,1,1]{2,1,0:T(1,128)S(1)} async-done(((f32[32,1,1]{2,1,0:T(1,128)}), f32[32,1,1]{2,1,0:T(1,128)S(1)}, u32[]{:S(2)}, u32[]{:S(2)}) %all-to-all-start.5) | async-done | bytes 160 | tf_op jit(solution)/shard_map/all_to_all | solution.py:19
  203.7 0.8 reduce.12
  (44 shorter events, 1.0 us)
Async XLA Ops:
  3.3 24.6 %all-to-all-start = ((bf16[32,32,256]{2,1,0:T(8,128)(2,1)}), bf16[32,32,256]{2,1,0:T(8,128)(2,1)S(1)}, u32[]{:S(2)}, u32[]{:S(2)}) async-start(bf16[32,32,256]{2,1,0:T(8,128)(2,1)} %add_convert_fusion.3), calls=%async_computation | async-start | bytes 1048576 | tf_op jit(solution)/shard_map/all_to_all | solution.py:66
  27.9 42.4 %all-to-all-start.1 = ((bf16[32,72,256]{2,1,0:T(8,128)(2,1)}), bf16[32,72,256]{2,1,0:T(8,128)(2,1)S(1)}, u32[]{:S(2)}, u32[]{:S(2)}) async-start(bf16[32,72,256]{2,1,0:T(8,128)(2,1)} %add_convert_fusion.1), calls=%async_computation.1 | async-start | bytes 2359296 | tf_op jit(solution)/shard_map/all_to_all | solution.py:66
  60.8 9.6 %copy-start.4 = (f32[256]{0:T(256)}, f32[256]{0:T(256)S(1)}, u32[]{:S(2)}) copy-start(f32[256]{0:T(256)S(1)} %get-tuple-element.45) | copy-start | bytes 3076
  70.4 45.9 %all-to-all-start.2 = ((bf16[32,8,1024]{2,1,0:T(8,128)(2,1)}), bf16[32,8,1024]{2,1,0:T(8,128)(2,1)S(1)}, u32[]{:S(2)}, u32[]{:S(2)}) async-start(bf16[32,8,1024]{2,1,0:T(8,128)(2,1)} %add_convert_fusion.2), calls=%async_computation.2 | async-start | bytes 1048576 | tf_op jit(solution)/shard_map/all_to_all | solution.py:66
  80.4 7.3 %copy-start = (bf16[32,16,14,256]{3,0,2,1:T(8,128)(2,1)S(1)}, bf16[32,16,14,256]{3,0,2,1:T(8,128)(2,1)}, u32[]{:S(2)}) copy-start(bf16[32,16,14,256]{3,0,2,1:T(8,128)(2,1)} %get-tuple-element.15) | copy-start | bytes 11010052
  80.4 8.4 %copy-start.1 = (bf16[32,16,14,256]{3,0,2,1:T(8,128)(2,1)S(1)}, bf16[32,16,14,256]{3,0,2,1:T(8,128)(2,1)}, u32[]{:S(2)}) copy-start(bf16[32,16,14,256]{3,0,2,1:T(8,128)(2,1)} %get-tuple-element.16) | copy-start | bytes 11010052
  80.4 9.4 %copy-start.2 = (bf16[32,16,14,256]{3,0,2,1:T(8,128)(2,1)S(1)}, bf16[32,16,14,256]{3,0,2,1:T(8,128)(2,1)}, u32[]{:S(2)}) copy-start(bf16[32,16,14,256]{3,0,2,1:T(8,128)(2,1)} %get-tuple-element.17) | copy-start | bytes 11010052
  116.3 77.8 %copy-start.5 = (f32[256]{0:T(256)}, f32[256]{0:T(256)S(1)}, u32[]{:S(2)}) copy-start(f32[256]{0:T(256)S(1)} %get-tuple-element.42) | copy-start | bytes 3076
  116.3 51.8 %all-to-all-start.3 = ((bf16[32,1000,32]{1,2,0:T(8,128)(2,1)}), bf16[32,1000,32]{1,2,0:T(8,128)(2,1)S(1)}, u32[]{:S(2)}, u32[]{:S(2)}) async-start(bf16[32,1000,32]{1,2,0:T(8,128)(2,1)} %add_convert_fusion), calls=%async_computation.3 | async-start | bytes 4194304 | tf_op jit(solution)/shard_map/all_to_all | solution.py:64
  152.8 15.4 %copy-start.3 = (f32[1024]{0:T(1024)}, f32[1024]{0:T(1024)S(1)}, u32[]{:S(2)}) copy-start(f32[1024]{0:T(1024)S(1)} %get-tuple-element.36) | copy-start | bytes 12292
  153.4 14.8 %copy-start.6 = (s32[32]{0:T(128)S(1)}, s32[32]{0:T(128)}, u32[]{:S(2)}) copy-start(s32[32]{0:T(128)} %param.12) | copy-start | bytes 388
  178.0 25.7 %all-to-all-start.5 = ((f32[32,1,1]{2,1,0:T(1,128)}), f32[32,1,1]{2,1,0:T(1,128)S(1)}, u32[]{:S(2)}, u32[]{:S(2)}) async-start(f32[32,1,1]{2,1,0:T(1,128)} %broadcast_in_dim.27), calls=%async_computation.5 | async-start | bytes 32768 | tf_op jit(solution)/shard_map/all_to_all | solution.py:19
